TPU v7x, 512 devices: a whole 4x8x8 slice. The times are simulated.
512 devices in a mesh: row: 16 (over y, core), col: 32 (over z, x).
Axes of the slice: x: 4, y: 8, z: 8, core: 2. Of those that a mesh axis runs over, the one named last changes fastest.
Arguments:
- offsets: float32 [3, 131072], P(None, ('row', 'col')), may hold values from 0 to 11
- cells: int32 [3, 1024], replicated, may hold values from 0 to 15, as said below
- types: int32 [131072], P(('row', 'col')), may hold values from 0 to 3, as said below
- mask: int32 [16, 64, 16, 64], P(None, 'col', 'row'), may hold values from 0 to 1, as said below
- chi_table: float32 [4], replicated, may hold values from 2 to 10.1
- eta_table: float32 [4], replicated, may hold values from 13 to 18
- gamma_table: float32 [4], replicated, may hold values from 0.4 to 0.8
Outputs:
- charges: float32 [131072], P(('row', 'col'))
Inputs may be any that keep to these rules, and one draw needn't show every extreme that they name: The cells of the blocks are a permutation of all 16 x 16 x 4 cells: each cell holds exactly one block. The mask marks a pair of blocks exactly when their cells are equal or adjacent on the periodic grid in every dimension; it is symmetric and each block is marked with exactly 27 blocks, itself included. `types`: types 2 and 3 grow more common along the atoms, from none in the first 256 atoms to nearly all in the last.
All inputs are finite; a program needn't handle non-finite values.
Results may differ from a plain program's by a relative error of at most 0.0003.
Values sent between devices are 32-bit elements; how exact they have to be, the bound alone decides.
A program may use at most 64 MiB of HBM per device.

v0:
```python
import jax
import jax.numpy as jnp
from jax import lax
from jax.sharding import Mesh
from jax.sharding import PartitionSpec as P

BLOCK = 128
GRID_Z = 4
ITERS = 3
ROW_COL = ("row_0", "row_1", "col_0", "col_1")
ROW = ("row_0", "row_1")
COL = ("col_0", "col_1")
coulomb = 14.4
cutoff = 10.0
cell_side = 11.0
pair_group = 64


def copy_for_each(value, axis):
    devices = lax.axis_size(axis)
    return lax.all_to_all(
        jnp.broadcast_to(value[None], (devices, *value.shape)), axis, 0, 0, tiled=True
    )


def over_copies(value, axis):
    return copy_for_each(value, axis).sum(axis=0)


def over_axes(value, axes):
    far, near = axes
    return over_copies(over_copies(value, near), far)


def in_one(arrays, axis):
    line, at, outs = (jnp.concatenate([a.reshape(-1) for a in arrays]), 0, [])
    subtotal = over_axes(line, axis)
    for a in arrays:
        outs.append(subtotal[at : at + a.size].reshape(a.shape))
        at += a.size
    return tuple(outs)


def in_order(blocks, dim):
    blocks = jnp.moveaxis(blocks, 0, dim)
    lengths = blocks.shape
    return blocks.reshape(*lengths[:dim], lengths[dim] * lengths[dim + 1], *lengths[dim + 2 :])


def gathered_copies(value, axis, dim):
    return in_order(copy_for_each(value, axis), dim)


def in_blocks(value, dim, devices):
    before, after = (value.shape[:dim], value.shape[dim + 1 :])
    return jnp.moveaxis(value.reshape(*before, devices, -1, *after), dim, 0)


def sent_and_summed(value, axis, dim):
    devices = lax.axis_size(axis)
    blocks = lax.all_to_all(in_blocks(value, dim, devices), axis, 0, 0, tiled=True)
    return jnp.sum(blocks, axis=0)


def taper(dist):
    xval = dist / cutoff
    poly = 1.0 + xval**4 * (-35.0 + xval * (84.0 + xval * (-70.0 + 20.0 * xval)))
    return jnp.where(xval < 1.0, poly, 0.0)


def coupling(tgt, src, tgt_cell, src_cell, same, grid):
    half = grid[:, None] // 2
    shift = ((src_cell - tgt_cell + half) % grid[:, None] - half).astype(jnp.float32) * cell_side
    radius_sq = jnp.zeros((tgt.shape[1], tgt.shape[2], src.shape[2]), jnp.float32)
    for comp in range(3):
        delta = shift[comp][:, None, None] + src[comp][:, None, :] - tgt[comp][:, :, None]
        radius_sq = radius_sq + delta * delta
    dist = jnp.sqrt(radius_sq)
    paired = tgt[3][:, :, None] * src[3][:, None, :]
    shield = 1.0 / (paired * jnp.sqrt(paired))
    kern = coulomb * taper(dist) / jnp.cbrt(radius_sq * dist + shield)
    width = tgt.shape[2]
    diag = jnp.arange(width)[:, None] == jnp.arange(width)[None, :]
    return jnp.where(same[:, None, None] & diag[None], 0.0, kern)


def pick(kinds, table):
    return jnp.sum(jnp.where(kinds, table[:, None], 0.0), axis=0)


def paired_sums(residual, image):
    return in_one(
        (jnp.sum(residual * residual, axis=1), jnp.sum(residual * image, axis=1)),
        ("row_0", ("row_1", "col_0", "col_1")),
    )


def per_device(offsets, cells, types, mask, chi_table, eta_table, gamma_table):
    n_row = lax.axis_size(ROW)
    n_col = lax.axis_size(COL)
    row_at = lax.axis_index(ROW)
    col_at = lax.axis_index(COL)
    span = types.shape[0]
    bpd = span // BLOCK
    n_tgt = n_row * bpd
    n_src = n_col * bpd
    grid = jnp.array([n_row, n_src // GRID_Z, GRID_Z], jnp.int32)
    kinds = jnp.arange(chi_table.shape[0])[:, None] == types[None, :]
    chi = pick(kinds, chi_table)
    eta = pick(kinds, eta_table)
    gamma = pick(kinds, gamma_table)
    geo = jnp.concatenate([offsets, gamma[None]], axis=0)
    src_geo = gathered_copies(geo, COL, 1).reshape(4, n_src, BLOCK)
    tgt_geo = lax.all_gather(geo, ROW, axis=1, tiled=True).reshape(4, n_tgt, BLOCK)
    tgt_ids = (
        (jnp.arange(n_row, dtype=jnp.int32)[:, None] * n_col + col_at) * bpd
        + jnp.arange(bpd, dtype=jnp.int32)[None, :]
    ).reshape(n_tgt)
    src_ids = row_at * n_src + jnp.arange(n_src, dtype=jnp.int32)
    tgt_cells = jnp.take(cells, tgt_ids, axis=1)
    src_cells = jnp.take(cells, src_ids, axis=1)
    tile = mask.reshape(n_tgt * n_src)
    count = jnp.sum(tile)
    slots = jnp.nonzero(tile, size=n_tgt * n_src + pair_group, fill_value=0)[0].astype(jnp.int32)
    groups = (count + pair_group - 1) // pair_group
    src_range = jnp.arange(n_src, dtype=jnp.int32)

    def block_kernel(step):
        picked = lax.dynamic_slice_in_dim(slots, step * pair_group, pair_group)
        live = step * pair_group + jnp.arange(pair_group) < count
        tgt_blk = picked // n_src
        src_blk = picked % n_src
        kern = coupling(
            tgt_geo[:, tgt_blk],
            src_geo[:, src_blk],
            tgt_cells[:, tgt_blk],
            src_cells[:, src_blk],
            tgt_ids[tgt_blk] == src_ids[src_blk],
            grid,
        )
        return (jnp.where(live[:, None, None], kern, 0.0), tgt_blk, src_blk)

    def apply(direction):
        remote = lax.all_gather(direction, ROW, axis=1, tiled=True).reshape(2, n_tgt, BLOCK)

        def turn(step, acc):
            kern, tgt_blk, src_blk = block_kernel(step)
            contrib = jnp.einsum(
                "gij,kgi->kgj", kern, remote[:, tgt_blk], precision=lax.Precision.HIGHEST
            )
            owners = (src_range[:, None] == src_blk[None, :]).astype(jnp.float32)
            return acc + jnp.einsum("sg,kgj->ksj", owners, contrib, precision=lax.Precision.HIGHEST)

        acc = lax.fori_loop(0, groups, turn, jnp.zeros((2, n_src, BLOCK), jnp.float32))
        summed = sent_and_summed(acc.reshape(2, n_src * BLOCK), COL, 1)
        return summed + eta[None] * direction

    rhs = jnp.stack([-chi, -jnp.ones_like(chi)], axis=0)
    solution = jnp.zeros_like(rhs)
    residual = rhs
    image = apply(residual)
    norm_now, product = paired_sums(residual, image)
    alpha = norm_now / product
    direction = residual
    along = image
    for step in range(ITERS):
        solution = solution + alpha[:, None] * direction
        residual = residual - alpha[:, None] * along
        if step + 1 < ITERS:
            image = apply(residual)
            norm_next, product = paired_sums(residual, image)
            ratio = norm_next / norm_now
            alpha = norm_next / (product - ratio * norm_next / alpha)
            direction = residual + ratio[:, None] * direction
            along = image + ratio[:, None] * along
            norm_now = norm_next
    totals = over_axes(jnp.sum(solution, axis=1), ("row_0", ("row_1", "col_0", "col_1")))
    return solution[0] - totals[0] / totals[1] * solution[1]


def solution(mesh):
    torus = Mesh(mesh.devices.reshape(8, 2, 8, 4), ("row_0", "row_1", "col_0", "col_1"))
    placed = (P(None, ROW_COL), P(), P(ROW_COL), P(None, COL, ROW, None), P(), P(), P())
    return jax.shard_map(
        per_device, mesh=torus, in_specs=placed, out_specs=P(ROW_COL), check_vma=False
    )
```

profile of v0, /device:TPU:1, one launch (start us, length us, event | category | flops | bytes accessed | tf_op | source)
XLA Modules:
  0.0 372.8 jit_solution(4462579200094896409)
XLA Ops:
  0.0 0.8 select_reduce_fusion
  0.8 0.7 pad_maximum_fusion
  1.5 0.7 broadcast_in_dim.293
  2.2 13.7 %all-to-all-start = ((f32[32,4,256]{2,1,0:T(4,128)}), f32[32,4,256]{2,1,0:T(4,128)S(1)}, u32[]{:S(2)}, u32[]{:S(2)}) async-start(f32[32,4,256]{2,1,0:T(4,128)} %broadcast_in_dim.293), calls=%async_computation | async-start | bytes 262144 | tf_op jit(solution)/shard_map/all_to_all | solution.py:21
  15.9 1.4 fusion.201
  18.5 0.6 gather_fusion.21
  19.1 0.6 gather_fusion.22
  19.8 0.3 reduce-window.16
  20.4 14.7 %scatter_custom_fusion = s32[2112]{0:T(1024)S(1)} fusion(s32[2048]{0:T(1024)S(1)} %bitcast.241, s32[2048]{0:T(1024)S(1)} %broadcast.958, s32[]{:T(128)} %constant.520.clone.1), kind=kCustom, calls=%fused_computation.302 | custom fusion | flops 2048 | bytes 8452 | tf_op jit(solution)/shard_map/scatter-add | solution.py:124
  35.7 18.5 %all_gather.12 = f32[2,4096]{1,0:T(2,128)S(1)} all-gather(f32[2,256]{1,0:T(2,128)S(1)} %stack.2), channel_id=1, replica_groups=mesh['row_0'=8,'row_1'=2,'col_0'=8,'col_1'=4] {'row_0','row_1'}, dimensions={1}, use_global_device_ids=true | all-gather | bytes 34816 | tf_op jit(solution)/shard_map/all_gather | solution.py:144
  54.2 0.7 fusion.199
  54.9 15.1 %all_gather.13 = f32[4,4096]{1,0:T(4,128)S(1)} all-gather(f32[4,256]{1,0:T(4,128)S(1)} %pad_maximum_fusion), channel_id=1, replica_groups=mesh['row_0'=8,'row_1'=2,'col_0'=8,'col_1'=4] {'row_0','row_1'}, dimensions={1}, use_global_device_ids=true | all-gather | bytes 69632 | tf_op jit(solution)/shard_map/all_gather | solution.py:114
  70.1 21.0 %while.48 = (s32[]{:T(128)}, f32[2,64,128]{2,1,0:T(8,128)S(1)}, s32[]{:T(128)}, s32[2112]{0:T(1024)S(1)}, f32[2,32,128]{2,0,1:T(2,128)S(1)}, /*index=5*/s32[]{:T...) while((s32[]{:T(128)}, f32[2,64,128]{2,1,0:T(8,128)S(1)}, ...), condition=%wide.region_11.13_spmd.clone.clone.clone, body=%wide.region_10.12_spmd.sunk.clone.clone.clone.sunk | while | flops 70322144 | bytes 2021583 | solution.py:154
  70.3 0.6 gather_fusion.2
  70.9 0.6 gather_fusion.3
  71.5 0.4 fusion.248
  72.0 0.7 gather_fusion
  73.0 0.8 gather_fusion.5
  74.0 0.8 gather_fusion.4
  74.8 0.7 gather_fusion.1
  75.5 0.7 gather_fusion.6
  76.2 0.6 add_compare_fusion.6
  76.8 14.2 %fusion.249 = f32[2,64,128]{2,0,1:T(2,128)S(1)} fusion(f32[64,128]{1,0:T(8,128)S(1)} %bitcast.216, f32[64,128]{1,0:T(8,128)S(1)} %bitcast.222, f32[64,128]{1,0:T(8,128)S(1)} %bitcast.220, f32[64,128]{1,0:T(8,128)S(1)} %broadcast_add_fusion.19, f32[64,128]{1,0:T(8,128)S(1)} %bitcast.221, f32[64,128]{1,0:T(8,128)S(1)} %broadcast_add_fusion.20, ...), kind=kOutput, calls=%fused_computation.77.clone.1 | convolution fusion | flops 57671680 | bytes 409728 | tf_op jit(solution)/shard_map/while/body/gij,kgi->kgj/dot_general | solution.py:148
  91.3 18.1 %all_to_all.68 = f32[32,2,256]{2,1,0:T(2,128)S(1)} all-to-all(f32[32,2,256]{2,1,0:T(2,128)S(1)} %copy.39), channel_id=1, replica_groups=mesh['row_0'=8,'row_1'=2,'col_0'=8,'col_1'=4] {'col_0','col_1'}, dimensions={0} | all-to-all | bytes 131072 | tf_op jit(solution)/shard_map/all_to_all | solution.py:61
  109.7 14.1 %all_to_all.69 = f32[64,1,4]{2,1,0:T(1,128)S(1)} all-to-all(f32[64,1,4]{2,1,0:T(1,128)S(1)} %broadcast_in_dim.295), channel_id=1, replica_groups=mesh['row_0'=8,'row_1'=2,'col_0'=8,'col_1'=4] {'row_1','col_0','col_1'}, dimensions={0} | all-to-all | bytes 2048 | tf_op jit(solution)/shard_map/all_to_all | solution.py:21
  123.9 0.6 broadcast_in_dim.296
  124.5 24.5 %all-to-all-start.3 = ((f32[8,1,4]{2,1,0:T(1,128)}), f32[8,1,4]{2,1,0:T(1,128)S(1)}, u32[]{:S(2)}, u32[]{:S(2)}) async-start(f32[8,1,4]{2,1,0:T(1,128)} %broadcast_in_dim.296), calls=%async_computation.3 | async-start | bytes 8192 | tf_op jit(solution)/shard_map/all_to_all | solution.py:21
  149.1 6.6 %all-to-all-done.3 = f32[8,1,4]{2,1,0:T(1,128)S(1)} async-done(((f32[8,1,4]{2,1,0:T(1,128)}), f32[8,1,4]{2,1,0:T(1,128)S(1)}, u32[]{:S(2)}, u32[]{:S(2)}) %all-to-all-start.3) | async-done | bytes 160 | tf_op jit(solution)/shard_map/all_to_all | solution.py:21
  155.8 16.5 %all_gather.14 = f32[2,4096]{1,0:T(2,128)S(1)} all-gather(f32[2,256]{1,0:T(2,128)S(1)} %multiply_subtract_fusion.1), channel_id=1, replica_groups=mesh['row_0'=8,'row_1'=2,'col_0'=8,'col_1'=4] {'row_0','row_1'}, dimensions={1}, use_global_device_ids=true | all-gather | bytes 34816 | tf_op jit(solution)/shard_map/all_gather | solution.py:144
  172.4 21.0 %while.49 = (s32[]{:T(128)}, f32[2,64,128]{2,1,0:T(8,128)S(1)}, s32[]{:T(128)}, s32[2112]{0:T(1024)S(1)}, f32[2,32,128]{2,0,1:T(2,128)S(1)}, /*index=5*/s32[]{:T...) while((s32[]{:T(128)}, f32[2,64,128]{2,1,0:T(8,128)S(1)}, ...), condition=%wide.region_19.21_spmd.clone.clone.clone, body=%wide.region_18.20_spmd.sunk.clone.clone.clone.sunk | while | flops 70322144 | bytes 2021583 | solution.py:154
  172.5 0.6 gather_fusion.9
  173.1 0.6 gather_fusion.10
  173.7 0.4 fusion.257
  174.2 0.7 gather_fusion.7
  175.2 0.8 gather_fusion.12
  176.2 0.8 gather_fusion.11
  177.0 0.7 gather_fusion.8
  177.7 0.7 gather_fusion.13
  178.4 0.6 add_compare_fusion.7
  179.0 14.2 %fusion.258 = f32[2,64,128]{2,0,1:T(2,128)S(1)} fusion(f32[64,128]{1,0:T(8,128)S(1)} %bitcast.217, f32[64,128]{1,0:T(8,128)S(1)} %bitcast.226, f32[64,128]{1,0:T(8,128)S(1)} %bitcast.224, f32[64,128]{1,0:T(8,128)S(1)} %broadcast_add_fusion.22, f32[64,128]{1,0:T(8,128)S(1)} %bitcast.225, f32[64,128]{1,0:T(8,128)S(1)} %broadcast_add_fusion.23, ...), kind=kOutput, calls=%fused_computation.161.clone.1 | convolution fusion | flops 57671680 | bytes 409728 | tf_op jit(solution)/shard_map/while/body/gij,kgi->kgj/dot_general | solution.py:148
  193.5 11.8 %all_to_all.70 = f32[32,2,256]{2,1,0:T(2,128)S(1)} all-to-all(f32[32,2,256]{2,1,0:T(2,128)S(1)} %copy.42), channel_id=1, replica_groups=mesh['row_0'=8,'row_1'=2,'col_0'=8,'col_1'=4] {'col_0','col_1'}, dimensions={0} | all-to-all | bytes 131072 | tf_op jit(solution)/shard_map/all_to_all | solution.py:61
  205.7 14.0 %all_to_all.71 = f32[64,1,4]{2,1,0:T(1,128)S(1)} all-to-all(f32[64,1,4]{2,1,0:T(1,128)S(1)} %broadcast_in_dim.297), channel_id=1, replica_groups=mesh['row_0'=8,'row_1'=2,'col_0'=8,'col_1'=4] {'row_1','col_0','col_1'}, dimensions={0} | all-to-all | bytes 2048 | tf_op jit(solution)/shard_map/all_to_all | solution.py:21
  219.7 0.6 broadcast_in_dim.298
  220.3 24.5 %all-to-all-start.6 = ((f32[8,1,4]{2,1,0:T(1,128)}), f32[8,1,4]{2,1,0:T(1,128)S(1)}, u32[]{:S(2)}, u32[]{:S(2)}) async-start(f32[8,1,4]{2,1,0:T(1,128)} %broadcast_in_dim.298), calls=%async_computation.6 | async-start | bytes 8192 | tf_op jit(solution)/shard_map/all_to_all | solution.py:21
  244.8 6.6 %all-to-all-done.6 = f32[8,1,4]{2,1,0:T(1,128)S(1)} async-done(((f32[8,1,4]{2,1,0:T(1,128)}), f32[8,1,4]{2,1,0:T(1,128)S(1)}, u32[]{:S(2)}, u32[]{:S(2)}) %all-to-all-start.6) | async-done | bytes 160 | tf_op jit(solution)/shard_map/all_to_all | solution.py:21
  251.6 16.5 %all_gather.15 = f32[2,4096]{1,0:T(2,128)S(1)} all-gather(f32[2,256]{1,0:T(2,128)S(1)} %multiply_subtract_fusion), channel_id=1, replica_groups=mesh['row_0'=8,'row_1'=2,'col_0'=8,'col_1'=4] {'row_0','row_1'}, dimensions={1}, use_global_device_ids=true | all-gather | bytes 34816 | tf_op jit(solution)/shard_map/all_gather | solution.py:144
  268.1 21.0 %while.50 = (s32[]{:T(128)}, f32[2,64,128]{2,1,0:T(8,128)S(1)}, s32[]{:T(128)}, s32[2112]{0:T(1024)S(1)}, f32[2,32,128]{2,0,1:T(2,128)S(1)}, /*index=5*/s32[]{:T...) while((s32[]{:T(128)}, f32[2,64,128]{2,1,0:T(8,128)S(1)}, ...), condition=%wide.region_26.28_spmd.clone.clone.clone, body=%wide.region_25.27_spmd.sunk.clone.clone.clone.sunk | while | flops 70322144 | bytes 2021583 | solution.py:154
  268.2 0.6 gather_fusion.16
  268.8 0.6 gather_fusion.17
  269.4 0.4 fusion.266
  270.0 0.7 gather_fusion.14
  271.0 0.8 gather_fusion.19
  271.9 0.8 gather_fusion.18
  272.7 0.7 gather_fusion.15
  273.5 0.7 gather_fusion.20
  274.1 0.6 add_compare_fusion.8
  274.7 14.2 %fusion.267 = f32[2,64,128]{2,0,1:T(2,128)S(1)} fusion(f32[64,128]{1,0:T(8,128)S(1)} %bitcast.218, f32[64,128]{1,0:T(8,128)S(1)} %bitcast.230, f32[64,128]{1,0:T(8,128)S(1)} %bitcast.228, f32[64,128]{1,0:T(8,128)S(1)} %broadcast_add_fusion.25, f32[64,128]{1,0:T(8,128)S(1)} %bitcast.229, f32[64,128]{1,0:T(8,128)S(1)} %broadcast_add_fusion.26, ...), kind=kOutput, calls=%fused_computation.245.clone.1 | convolution fusion | flops 57671680 | bytes 409728 | tf_op jit(solution)/shard_map/while/body/gij,kgi->kgj/dot_general | solution.py:148
  289.2 11.8 %all_to_all.72 = f32[32,2,256]{2,1,0:T(2,128)S(1)} all-to-all(f32[32,2,256]{2,1,0:T(2,128)S(1)} %copy.45), channel_id=1, replica_groups=mesh['row_0'=8,'row_1'=2,'col_0'=8,'col_1'=4] {'col_0','col_1'}, dimensions={0} | all-to-all | bytes 131072 | tf_op jit(solution)/shard_map/all_to_all | solution.py:61
  301.4 14.0 %all_to_all.73 = f32[64,1,4]{2,1,0:T(1,128)S(1)} all-to-all(f32[64,1,4]{2,1,0:T(1,128)S(1)} %broadcast_in_dim.299), channel_id=1, replica_groups=mesh['row_0'=8,'row_1'=2,'col_0'=8,'col_1'=4] {'row_1','col_0','col_1'}, dimensions={0} | all-to-all | bytes 2048 | tf_op jit(solution)/shard_map/all_to_all | solution.py:21
  315.5 30.9 %all_to_all.74 = f32[8,1,4]{2,1,0:T(1,128)S(1)} all-to-all(f32[8,1,4]{2,1,0:T(1,128)S(1)} %broadcast_in_dim.300), channel_id=1, replica_groups=mesh['row_0'=8,'row_1'=2,'col_0'=8,'col_1'=4] {'row_0'}, dimensions={0} | all-to-all | bytes 256 | tf_op jit(solution)/shard_map/all_to_all | solution.py:21
  346.7 14.5 %all_to_all.75 = f32[64,1,2]{2,1,0:T(1,128)S(1)} all-to-all(f32[64,1,2]{2,1,0:T(1,128)S(1)} %broadcast_in_dim.301), channel_id=1, replica_groups=mesh['row_0'=8,'row_1'=2,'col_0'=8,'col_1'=4] {'row_1','col_0','col_1'}, dimensions={0} | all-to-all | bytes 1024 | tf_op jit(solution)/shard_map/all_to_all | solution.py:21
  361.3 8.9 %all_to_all.76 = f32[8,1,2]{2,1,0:T(1,128)S(1)} all-to-all(f32[8,1,2]{2,1,0:T(1,128)S(1)} %broadcast_in_dim.302), channel_id=1, replica_groups=mesh['row_0'=8,'row_1'=2,'col_0'=8,'col_1'=4] {'row_0'}, dimensions={0} | all-to-all | bytes 128 | tf_op jit(solution)/shard_map/all_to_all | solution.py:21
  370.2 0.6 fusion.214
  372.2 0.6 fusion.204
  (120 shorter events, 7.1 us)
Async XLA Ops:
  0.0 18.2 %copy-start.3 = (s32[3,1024]{1,0:T(4,128)S(1)}, s32[3,1024]{1,0:T(4,128)}, u32[]{:S(2)}) copy-start(s32[3,1024]{1,0:T(4,128)} %param.17) | copy-start | bytes 36868
  2.2 67.9 %all-to-all-start = ((f32[32,4,256]{2,1,0:T(4,128)}), f32[32,4,256]{2,1,0:T(4,128)S(1)}, u32[]{:S(2)}, u32[]{:S(2)}) async-start(f32[32,4,256]{2,1,0:T(4,128)} %broadcast_in_dim.293), calls=%async_computation | async-start | bytes 262144 | tf_op jit(solution)/shard_map/all_to_all | solution.py:21
  18.2 51.9 %copy-start = (s32[3]{0:T(128)S(1)}, s32[3]{0:T(128)}, u32[]{:S(2)}) copy-start(s32[3]{0:T(128)} %constant.962) | copy-start | bytes 40
  18.2 51.9 %copy-start.1 = (s32[3]{0:T(128)S(1)}, s32[3]{0:T(128)}, u32[]{:S(2)}) copy-start(s32[3]{0:T(128)} %constant.963) | copy-start | bytes 40
  18.2 51.9 %copy-start.2 = (s32[3]{0:T(128)S(1)}, s32[3]{0:T(128)}, u32[]{:S(2)}) copy-start(s32[3]{0:T(128)} %constant.964) | copy-start | bytes 40
  124.5 31.1 %all-to-all-start.3 = ((f32[8,1,4]{2,1,0:T(1,128)}), f32[8,1,4]{2,1,0:T(1,128)S(1)}, u32[]{:S(2)}, u32[]{:S(2)}) async-start(f32[8,1,4]{2,1,0:T(1,128)} %broadcast_in_dim.296), calls=%async_computation.3 | async-start | bytes 8192 | tf_op jit(solution)/shard_map/all_to_all | solution.py:21
  220.3 31.1 %all-to-all-start.6 = ((f32[8,1,4]{2,1,0:T(1,128)}), f32[8,1,4]{2,1,0:T(1,128)S(1)}, u32[]{:S(2)}, u32[]{:S(2)}) async-start(f32[8,1,4]{2,1,0:T(1,128)} %broadcast_in_dim.298), calls=%async_computation.6 | async-start | bytes 8192 | tf_op jit(solution)/shard_map/all_to_all | solution.py:21
where the time goes:
time: 374 us; the launch traced here: 373 us
  blocking collectives  205 us (55%)
  starting transfers between devices  62.8 us (17%)
  matrix products  43.2 us (12%)
  other arithmetic  25.8 us (7%)
  local copies, waits for them, and re-layouts  20.5 us (5%)
  waiting for transfers between devices  13.1 us (4%)
    all_to_all x6, blocking collectives, copy_for_each(): lax.all_to_all(jnp.broadcast_to(value[None], (devices, *value.shape)), ax...  96.4 us
    all_to_all x3, starting transfers between devices, copy_for_each(): lax.all_to_all(jnp.broadcast_to(value[None], (devices, *value.shape)), ax...  62.8 us
    all_gather x3, blocking collectives, apply(): lax.all_gather(direction, ROW, axis=1, tiled=True).reshape(2, n_tgt, BLOCK)  51.5 us
    dot_general x3, matrix products, turn(): jnp.einsum('gij,kgi->kgj', kern, remote[:, tgt_blk], precision=lax.Precis...  42.6 us
    all_to_all x3, blocking collectives, sent_and_summed(): lax.all_to_all(in_blocks(value, dim, devices), axis, 0, 0, tiled=True)  41.8 us
    all_gather x1, blocking collectives, per_device(): lax.all_gather(geo, ROW, axis=1, tiled=True).reshape(4, n_tgt, BLOCK)  15.1 us
    scatter-add x1, other arithmetic, per_device(): jnp.nonzero(tile, size=n_tgt * n_src + pair_group, fill_value=0)[0]  14.7 us
    all_to_all x3, waiting for transfers between devices, copy_for_each(): lax.all_to_all(jnp.broadcast_to(value[None], (devices, *value.shape)), ax...  13.1 us
  transfers between devices with their start and end apart: 3, of which 2 were waited for; matrix products, arithmetic and copies ran while one was open for 5% of the time, Pallas kernels for 0%

commit v1 on v0

--- a/solution.py
+++ b/solution.py
@@ -14,6 +14,11 @@
 cutoff = 10.0
 cell_side = 11.0
 pair_group = 64
+
+
+def gathered_along(value, mesh_axis, along):
+    parts = lax.all_gather(value, mesh_axis)
+    return jnp.concatenate(parts, axis=along)
 
 
 def copy_for_each(value, axis):
@@ -141,7 +146,7 @@
         return (jnp.where(live[:, None, None], kern, 0.0), tgt_blk, src_blk)
 
     def apply(direction):
-        remote = lax.all_gather(direction, ROW, axis=1, tiled=True).reshape(2, n_tgt, BLOCK)
+        remote = gathered_along(direction, ROW, 1).reshape(2, n_tgt, BLOCK)
 
         def turn(step, acc):
             kern, tgt_blk, src_blk = block_kernel(step)

time: 374 us -> 374 us (level)
  no operation moved by 1% of the time
where the time goes in v1:
time: 374 us; the launch traced here: 373 us
  blocking collectives  205 us (55%)
  starting transfers between devices  62.8 us (17%)
  matrix products  43.2 us (12%)
  other arithmetic  25.8 us (7%)
  local copies, waits for them, and re-layouts  20.5 us (5%)
  waiting for transfers between devices  13.1 us (4%)
    all_to_all x6, blocking collectives, copy_for_each(): lax.all_to_all(jnp.broadcast_to(value[None], (devices, *value.shape)), ax...  96.4 us
    all_to_all x3, starting transfers between devices, copy_for_each(): lax.all_to_all(jnp.broadcast_to(value[None], (devices, *value.shape)), ax...  62.8 us
    all_gather x3, blocking collectives, gathered_along(): parts = lax.all_gather(value, mesh_axis)  51.5 us
    dot_general x3, matrix products, turn(): jnp.einsum('gij,kgi->kgj', kern, remote[:, tgt_blk], precision=lax.Precis...  42.6 us
    all_to_all x3, blocking collectives, sent_and_summed(): lax.all_to_all(in_blocks(value, dim, devices), axis, 0, 0, tiled=True)  41.8 us
    all_gather x1, blocking collectives, per_device(): lax.all_gather(geo, ROW, axis=1, tiled=True).reshape(4, n_tgt, BLOCK)  15.1 us
    scatter-add x1, other arithmetic, per_device(): jnp.nonzero(tile, size=n_tgt * n_src + pair_group, fill_value=0)[0]  14.7 us
    all_to_all x3, waiting for transfers between devices, copy_for_each(): lax.all_to_all(jnp.broadcast_to(value[None], (devices, *value.shape)), ax...  13.1 us
  transfers between devices with their start and end apart: 3, of which 2 were waited for; matrix products, arithmetic and copies ran while one was open for 5% of the time, Pallas kernels for 0%

profile of v1, /device:TPU:1, one launch (start us, length us, event | category | flops | bytes accessed | tf_op | source)
XLA Modules:
  0.0 372.8 jit_solution(16744334833945063564)
XLA Ops:
  0.0 0.8 select_reduce_fusion
  0.8 0.7 pad_maximum_fusion
  1.5 0.7 broadcast_in_dim.293
  2.2 13.7 %all-to-all-start = ((f32[32,4,256]{2,1,0:T(4,128)}), f32[32,4,256]{2,1,0:T(4,128)S(1)}, u32[]{:S(2)}, u32[]{:S(2)}) async-start(f32[32,4,256]{2,1,0:T(4,128)} %broadcast_in_dim.293), calls=%async_computation | async-start | bytes 262144 | tf_op jit(solution)/shard_map/all_to_all | solution.py:26
  15.9 1.4 fusion.201
  18.5 0.6 gather_fusion.21
  19.1 0.6 gather_fusion.22
  19.8 0.3 reduce-window.16
  20.4 14.7 %scatter_custom_fusion = s32[2112]{0:T(1024)S(1)} fusion(s32[2048]{0:T(1024)S(1)} %bitcast.253, s32[2048]{0:T(1024)S(1)} %broadcast.958, s32[]{:T(128)} %constant.520.clone.1), kind=kCustom, calls=%fused_computation.302 | custom fusion | flops 2048 | bytes 8452 | tf_op jit(solution)/shard_map/scatter-add | solution.py:129
  35.7 18.5 %all-gather.3 = f32[16,2,256]{2,1,0:T(2,128)S(1)} all-gather(f32[1,2,256]{2,1,0:T(2,128)S(1)} %pad_bitcast_fusion.1), channel_id=2, replica_groups=mesh['row_0'=8,'row_1'=2,'col_0'=8,'col_1'=4] {'row_0','row_1'}, dimensions={0}, use_global_device_ids=true | all-gather | bytes 34816 | tf_op jit(solution)/shard_map/all_gather | solution.py:20
  54.2 0.7 fusion.199
  54.9 15.1 %all_gather.23 = f32[4,4096]{1,0:T(4,128)S(1)} all-gather(f32[4,256]{1,0:T(4,128)S(1)} %pad_maximum_fusion), channel_id=1, replica_groups=mesh['row_0'=8,'row_1'=2,'col_0'=8,'col_1'=4] {'row_0','row_1'}, dimensions={1}, use_global_device_ids=true | all-gather | bytes 69632 | tf_op jit(solution)/shard_map/all_gather | solution.py:119
  70.1 21.0 %while.48 = (s32[]{:T(128)}, f32[2,64,128]{2,1,0:T(8,128)S(1)}, s32[]{:T(128)}, s32[2112]{0:T(1024)S(1)}, f32[2,32,128]{2,0,1:T(2,128)S(1)}, /*index=5*/s32[]{:T...) while((s32[]{:T(128)}, f32[2,64,128]{2,1,0:T(8,128)S(1)}, ...), condition=%wide.region_11.13_spmd.clone.clone.clone, body=%wide.region_10.12_spmd.sunk.clone.clone.clone.sunk | while | flops 70322144 | bytes 2021583 | solution.py:159
  70.3 0.6 gather_fusion.2
  70.9 0.6 gather_fusion.3
  71.5 0.4 fusion.256
  72.0 0.7 gather_fusion
  73.0 0.8 gather_fusion.5
  74.0 0.8 gather_fusion.4
  74.8 0.7 gather_fusion.1
  75.5 0.7 gather_fusion.6
  76.2 0.6 add_compare_fusion.6
  76.8 14.2 %fusion.257 = f32[2,64,128]{2,0,1:T(2,128)S(1)} fusion(f32[64,128]{1,0:T(8,128)S(1)} %bitcast.227, f32[64,128]{1,0:T(8,128)S(1)} %bitcast.233, f32[64,128]{1,0:T(8,128)S(1)} %bitcast.231, f32[64,128]{1,0:T(8,128)S(1)} %broadcast_add_fusion.19, f32[64,128]{1,0:T(8,128)S(1)} %bitcast.232, f32[64,128]{1,0:T(8,128)S(1)} %broadcast_add_fusion.20, ...), kind=kOutput, calls=%fused_computation.77.clone.1 | convolution fusion | flops 57671680 | bytes 409728 | tf_op jit(solution)/shard_map/while/body/gij,kgi->kgj/dot_general | solution.py:153
  91.3 18.1 %all_to_all.68 = f32[32,2,256]{2,1,0:T(2,128)S(1)} all-to-all(f32[32,2,256]{2,1,0:T(2,128)S(1)} %copy.41), channel_id=1, replica_groups=mesh['row_0'=8,'row_1'=2,'col_0'=8,'col_1'=4] {'col_0','col_1'}, dimensions={0} | all-to-all | bytes 131072 | tf_op jit(solution)/shard_map/all_to_all | solution.py:66
  109.7 14.1 %all_to_all.69 = f32[64,1,4]{2,1,0:T(1,128)S(1)} all-to-all(f32[64,1,4]{2,1,0:T(1,128)S(1)} %broadcast_in_dim.295), channel_id=1, replica_groups=mesh['row_0'=8,'row_1'=2,'col_0'=8,'col_1'=4] {'row_1','col_0','col_1'}, dimensions={0} | all-to-all | bytes 2048 | tf_op jit(solution)/shard_map/all_to_all | solution.py:26
  123.9 0.6 broadcast_in_dim.296
  124.5 24.5 %all-to-all-start.3 = ((f32[8,1,4]{2,1,0:T(1,128)}), f32[8,1,4]{2,1,0:T(1,128)S(1)}, u32[]{:S(2)}, u32[]{:S(2)}) async-start(f32[8,1,4]{2,1,0:T(1,128)} %broadcast_in_dim.296), calls=%async_computation.3 | async-start | bytes 8192 | tf_op jit(solution)/shard_map/all_to_all | solution.py:26
  149.1 6.6 %all-to-all-done.3 = f32[8,1,4]{2,1,0:T(1,128)S(1)} async-done(((f32[8,1,4]{2,1,0:T(1,128)}), f32[8,1,4]{2,1,0:T(1,128)S(1)}, u32[]{:S(2)}, u32[]{:S(2)}) %all-to-all-start.3) | async-done | bytes 160 | tf_op jit(solution)/shard_map/all_to_all | solution.py:26
  155.8 16.5 %all-gather.4 = f32[16,2,256]{2,1,0:T(2,128)S(1)} all-gather(f32[1,2,256]{2,1,0:T(2,128)S(1)} %fusion.222), channel_id=3, replica_groups=mesh['row_0'=8,'row_1'=2,'col_0'=8,'col_1'=4] {'row_0','row_1'}, dimensions={0}, use_global_device_ids=true | all-gather | bytes 34816 | tf_op jit(solution)/shard_map/all_gather | solution.py:20
  172.4 21.0 %while.49 = (s32[]{:T(128)}, f32[2,64,128]{2,1,0:T(8,128)S(1)}, s32[]{:T(128)}, s32[2112]{0:T(1024)S(1)}, f32[2,32,128]{2,0,1:T(2,128)S(1)}, /*index=5*/s32[]{:T...) while((s32[]{:T(128)}, f32[2,64,128]{2,1,0:T(8,128)S(1)}, ...), condition=%wide.region_19.21_spmd.clone.clone.clone, body=%wide.region_18.20_spmd.sunk.clone.clone.clone.sunk | while | flops 70322144 | bytes 2021583 | solution.py:159
  172.5 0.6 gather_fusion.9
  173.1 0.6 gather_fusion.10
  173.7 0.4 fusion.265
  174.2 0.7 gather_fusion.7
  175.2 0.8 gather_fusion.12
  176.2 0.8 gather_fusion.11
  177.0 0.7 gather_fusion.8
  177.7 0.7 gather_fusion.13
  178.4 0.6 add_compare_fusion.7
  179.0 14.2 %fusion.266 = f32[2,64,128]{2,0,1:T(2,128)S(1)} fusion(f32[64,128]{1,0:T(8,128)S(1)} %bitcast.228, f32[64,128]{1,0:T(8,128)S(1)} %bitcast.237, f32[64,128]{1,0:T(8,128)S(1)} %bitcast.235, f32[64,128]{1,0:T(8,128)S(1)} %broadcast_add_fusion.22, f32[64,128]{1,0:T(8,128)S(1)} %bitcast.236, f32[64,128]{1,0:T(8,128)S(1)} %broadcast_add_fusion.23, ...), kind=kOutput, calls=%fused_computation.161.clone.1 | convolution fusion | flops 57671680 | bytes 409728 | tf_op jit(solution)/shard_map/while/body/gij,kgi->kgj/dot_general | solution.py:153
  193.5 11.8 %all_to_all.70 = f32[32,2,256]{2,1,0:T(2,128)S(1)} all-to-all(f32[32,2,256]{2,1,0:T(2,128)S(1)} %copy.44), channel_id=1, replica_groups=mesh['row_0'=8,'row_1'=2,'col_0'=8,'col_1'=4] {'col_0','col_1'}, dimensions={0} | all-to-all | bytes 131072 | tf_op jit(solution)/shard_map/all_to_all | solution.py:66
  205.7 14.0 %all_to_all.71 = f32[64,1,4]{2,1,0:T(1,128)S(1)} all-to-all(f32[64,1,4]{2,1,0:T(1,128)S(1)} %broadcast_in_dim.297), channel_id=1, replica_groups=mesh['row_0'=8,'row_1'=2,'col_0'=8,'col_1'=4] {'row_1','col_0','col_1'}, dimensions={0} | all-to-all | bytes 2048 | tf_op jit(solution)/shard_map/all_to_all | solution.py:26
  219.7 0.6 broadcast_in_dim.298
  220.3 24.5 %all-to-all-start.6 = ((f32[8,1,4]{2,1,0:T(1,128)}), f32[8,1,4]{2,1,0:T(1,128)S(1)}, u32[]{:S(2)}, u32[]{:S(2)}) async-start(f32[8,1,4]{2,1,0:T(1,128)} %broadcast_in_dim.298), calls=%async_computation.6 | async-start | bytes 8192 | tf_op jit(solution)/shard_map/all_to_all | solution.py:26
  244.8 6.6 %all-to-all-done.6 = f32[8,1,4]{2,1,0:T(1,128)S(1)} async-done(((f32[8,1,4]{2,1,0:T(1,128)}), f32[8,1,4]{2,1,0:T(1,128)S(1)}, u32[]{:S(2)}, u32[]{:S(2)}) %all-to-all-start.6) | async-done | bytes 160 | tf_op jit(solution)/shard_map/all_to_all | solution.py:26
  251.6 16.5 %all-gather.5 = f32[16,2,256]{2,1,0:T(2,128)S(1)} all-gather(f32[1,2,256]{2,1,0:T(2,128)S(1)} %bitcast.251), channel_id=4, replica_groups=mesh['row_0'=8,'row_1'=2,'col_0'=8,'col_1'=4] {'row_0','row_1'}, dimensions={0}, use_global_device_ids=true | all-gather | bytes 34816 | tf_op jit(solution)/shard_map/all_gather | solution.py:20
  268.1 21.0 %while.50 = (s32[]{:T(128)}, f32[2,64,128]{2,1,0:T(8,128)S(1)}, s32[]{:T(128)}, s32[2112]{0:T(1024)S(1)}, f32[2,32,128]{2,0,1:T(2,128)S(1)}, /*index=5*/s32[]{:T...) while((s32[]{:T(128)}, f32[2,64,128]{2,1,0:T(8,128)S(1)}, ...), condition=%wide.region_26.28_spmd.clone.clone.clone, body=%wide.region_25.27_spmd.sunk.clone.clone.clone.sunk | while | flops 70322144 | bytes 2021583 | solution.py:159
  268.2 0.6 gather_fusion.16
  268.8 0.6 gather_fusion.17
  269.4 0.4 fusion.274
  270.0 0.7 gather_fusion.14
  271.0 0.8 gather_fusion.19
  271.9 0.8 gather_fusion.18
  272.7 0.7 gather_fusion.15
  273.5 0.7 gather_fusion.20
  274.1 0.6 add_compare_fusion.8
  274.7 14.2 %fusion.275 = f32[2,64,128]{2,0,1:T(2,128)S(1)} fusion(f32[64,128]{1,0:T(8,128)S(1)} %bitcast.229, f32[64,128]{1,0:T(8,128)S(1)} %bitcast.241, f32[64,128]{1,0:T(8,128)S(1)} %bitcast.239, f32[64,128]{1,0:T(8,128)S(1)} %broadcast_add_fusion.25, f32[64,128]{1,0:T(8,128)S(1)} %bitcast.240, f32[64,128]{1,0:T(8,128)S(1)} %broadcast_add_fusion.26, ...), kind=kOutput, calls=%fused_computation.245.clone.1 | convolution fusion | flops 57671680 | bytes 409728 | tf_op jit(solution)/shard_map/while/body/gij,kgi->kgj/dot_general | solution.py:153
  289.2 11.8 %all_to_all.72 = f32[32,2,256]{2,1,0:T(2,128)S(1)} all-to-all(f32[32,2,256]{2,1,0:T(2,128)S(1)} %copy.47), channel_id=1, replica_groups=mesh['row_0'=8,'row_1'=2,'col_0'=8,'col_1'=4] {'col_0','col_1'}, dimensions={0} | all-to-all | bytes 131072 | tf_op jit(solution)/shard_map/all_to_all | solution.py:66
  301.4 14.0 %all_to_all.73 = f32[64,1,4]{2,1,0:T(1,128)S(1)} all-to-all(f32[64,1,4]{2,1,0:T(1,128)S(1)} %broadcast_in_dim.299), channel_id=1, replica_groups=mesh['row_0'=8,'row_1'=2,'col_0'=8,'col_1'=4] {'row_1','col_0','col_1'}, dimensions={0} | all-to-all | bytes 2048 | tf_op jit(solution)/shard_map/all_to_all | solution.py:26
  315.5 30.9 %all_to_all.74 = f32[8,1,4]{2,1,0:T(1,128)S(1)} all-to-all(f32[8,1,4]{2,1,0:T(1,128)S(1)} %broadcast_in_dim.300), channel_id=1, replica_groups=mesh['row_0'=8,'row_1'=2,'col_0'=8,'col_1'=4] {'row_0'}, dimensions={0} | all-to-all | bytes 256 | tf_op jit(solution)/shard_map/all_to_all | solution.py:26
  346.7 14.5 %all_to_all.75 = f32[64,1,2]{2,1,0:T(1,128)S(1)} all-to-all(f32[64,1,2]{2,1,0:T(1,128)S(1)} %broadcast_in_dim.301), channel_id=1, replica_groups=mesh['row_0'=8,'row_1'=2,'col_0'=8,'col_1'=4] {'row_1','col_0','col_1'}, dimensions={0} | all-to-all | bytes 1024 | tf_op jit(solution)/shard_map/all_to_all | solution.py:26
  361.3 8.9 %all_to_all.76 = f32[8,1,2]{2,1,0:T(1,128)S(1)} all-to-all(f32[8,1,2]{2,1,0:T(1,128)S(1)} %broadcast_in_dim.302), channel_id=1, replica_groups=mesh['row_0'=8,'row_1'=2,'col_0'=8,'col_1'=4] {'row_0'}, dimensions={0} | all-to-all | bytes 128 | tf_op jit(solution)/shard_map/all_to_all | solution.py:26
  370.2 0.6 fusion.221
  372.2 0.6 fusion.210
  (120 shorter events, 7.1 us)
Async XLA Ops:
  0.0 18.2 %copy-start.3 = (s32[3,1024]{1,0:T(4,128)S(1)}, s32[3,1024]{1,0:T(4,128)}, u32[]{:S(2)}) copy-start(s32[3,1024]{1,0:T(4,128)} %param.17) | copy-start | bytes 36868
  2.2 67.9 %all-to-all-start = ((f32[32,4,256]{2,1,0:T(4,128)}), f32[32,4,256]{2,1,0:T(4,128)S(1)}, u32[]{:S(2)}, u32[]{:S(2)}) async-start(f32[32,4,256]{2,1,0:T(4,128)} %broadcast_in_dim.293), calls=%async_computation | async-start | bytes 262144 | tf_op jit(solution)/shard_map/all_to_all | solution.py:26
  18.2 51.9 %copy-start = (s32[3]{0:T(128)S(1)}, s32[3]{0:T(128)}, u32[]{:S(2)}) copy-start(s32[3]{0:T(128)} %constant.970) | copy-start | bytes 40
  18.2 51.9 %copy-start.1 = (s32[3]{0:T(128)S(1)}, s32[3]{0:T(128)}, u32[]{:S(2)}) copy-start(s32[3]{0:T(128)} %constant.971) | copy-start | bytes 40
  18.2 51.9 %copy-start.2 = (s32[3]{0:T(128)S(1)}, s32[3]{0:T(128)}, u32[]{:S(2)}) copy-start(s32[3]{0:T(128)} %constant.972) | copy-start | bytes 40
  124.5 31.1 %all-to-all-start.3 = ((f32[8,1,4]{2,1,0:T(1,128)}), f32[8,1,4]{2,1,0:T(1,128)S(1)}, u32[]{:S(2)}, u32[]{:S(2)}) async-start(f32[8,1,4]{2,1,0:T(1,128)} %broadcast_in_dim.296), calls=%async_computation.3 | async-start | bytes 8192 | tf_op jit(solution)/shard_map/all_to_all | solution.py:26
  220.3 31.1 %all-to-all-start.6 = ((f32[8,1,4]{2,1,0:T(1,128)}), f32[8,1,4]{2,1,0:T(1,128)S(1)}, u32[]{:S(2)}, u32[]{:S(2)}) async-start(f32[8,1,4]{2,1,0:T(1,128)} %broadcast_in_dim.298), calls=%async_computation.6 | async-start | bytes 8192 | tf_op jit(solution)/shard_map/all_to_all | solution.py:26
